TPU v7x, 8 devices: a whole 2x2x1 slice. The times are simulated.
8 devices in a mesh: dp: 2 (over z, y), sp: 4 (over x, core).
Axes of the slice: x: 2, y: 2, z: 1, core: 2. Of those that a mesh axis runs over, the one named last changes fastest.
Arguments:
- hidden: bfloat16 [4096, 5120], P(('dp', 'sp')), parts along dimension 0
- ln_gain: bfloat16 [5120], replicated
- w_q: bfloat16 [5120, 8192], replicated
- w_k: bfloat16 [5120, 1024], replicated
- w_v: bfloat16 [5120, 1024], replicated
- w_o: bfloat16 [8192, 5120], replicated
- q_gain: bfloat16 [128], replicated
- k_gain: bfloat16 [128], replicated
Outputs:
- output: bfloat16 [4096, 5120], P(('dp', 'sp')), parts along dimension 0
There are 2 independent parts. A program takes and returns all parts, laid end to end along the dimension named above; an argument that names none is the same for every part.
All inputs are finite; a program needn't handle non-finite values.
Results may differ from a plain program's by a relative error of at most 0.00696765.
Values are sent between devices in bfloat16 or wider.
A program may use at most 1 GiB of HBM per device.

v0:
```python
import functools
import math

import jax
import jax.numpy as jnp
from jax import lax
from jax.experimental import pallas as pl
from jax.experimental.pallas import tpu as pltpu
from jax.sharding import PartitionSpec as P

EPS = 1e-6
THETA = 1000000.0
HD = 128
VMEM_LIMIT = 60 * 1024 * 1024
NT = (((1,), (1,)), ((), ()))
F32 = jnp.float32
BF16 = jnp.bfloat16
ANY = pl.BlockSpec(memory_space=pl.ANY)


def rope_tables(positions):
    half = HD // 2
    inv_freq = jnp.power(THETA, -(jnp.arange(half, dtype=F32) * (2.0 / HD)))
    angles = positions.astype(F32)[:, None] * inv_freq[None, :]
    cos = jnp.cos(angles)
    sin = jnp.sin(angles)
    return jnp.concatenate([cos, cos], axis=1), jnp.concatenate([-sin, sin], axis=1)


def front_kernel(x_hbm, g_ref, wq_hbm, wk_hbm, wv_hbm, cos_ref, sin_ref, qg_ref, kg_ref, q_out, k_out, v_out,
                 own_scr, part_scr, w_scr, ka_scr, va_scr, qa_scr, kv_st, q_st,
                 x_sems, w_sems, xs_sems, xr_sems, loc_sems, ps_sems, pr_sems, cs_sems, cr_sems, q_sems):
    sp = lax.axis_index('sp')
    chip = sp // 2
    core = sp % 2
    partner = chip * 2 + 1 - core
    rows, dim = x_hbm.shape
    bn = w_scr.shape[2]
    part_rows = rows // 4
    q_tiles = wq_hbm.shape[1] // 2 // bn

    def weight(src, col, slot):
        return pltpu.make_async_copy(src.at[:, pl.ds(pl.multiple_of(col, bn), bn)], w_scr.at[slot], w_sems.at[slot])

    def k_weight(s, slot):
        return weight(wk_hbm, (2 * core + s) % 4 * bn, slot)

    def v_weight(s, slot):
        return weight(wv_hbm, (2 * core + s) % 4 * bn, slot)

    def q_weight(n):
        return weight(wq_hbm, core * q_tiles * bn + n * bn, n % 4)

    def x_load(i):
        r = pl.ds(i * part_rows, part_rows)
        return pltpu.make_async_copy(x_hbm.at[r], own_scr.at[r], x_sems.at[i])

    def x_send(i):
        r = pl.ds(pl.multiple_of(i * part_rows, part_rows), part_rows)
        return pltpu.make_async_remote_copy(
            src_ref=x_hbm.at[r], dst_ref=part_scr.at[r], send_sem=xs_sems.at[i], recv_sem=xr_sems.at[i],
            device_id={'sp': partner}, device_id_type=pl.DeviceIdType.MESH)

    def norm(ref, i):
        width = 512
        for sub in range(part_rows // 16):
            r = pl.ds(pl.multiple_of(i * part_rows + sub * 16, 16), 16)
            total = None
            for lo in range(0, dim, width):
                x = ref[r, lo:lo + width].astype(F32)
                x = x * x
                for j in range(0, width, HD):
                    total = x[:, j:j + HD] if total is None else total + x[:, j:j + HD]
            inv = lax.rsqrt(jnp.sum(total, axis=1, keepdims=True) * (1.0 / dim) + EPS)
            for lo in range(0, dim, width):
                x = ref[r, lo:lo + width].astype(F32)
                ref[r, lo:lo + width] = (x * inv * g_ref[:, lo:lo + width].astype(F32)).astype(BF16)

    def rope(acc, at, gain_ref):
        var = jnp.mean(acc * acc, axis=-1, keepdims=True)
        t = acc * lax.rsqrt(var + EPS) * gain_ref[...].astype(F32)
        return t * cos_ref[at, :] + pltpu.roll(t, HD // 2, 1) * sin_ref[at, :]

    def kv_multiply(slot):
        ka_scr[...] = jnp.dot(own_scr[...], w_scr[slot], preferred_element_type=F32)
        va_scr[...] = jnp.dot(own_scr[...], w_scr[slot + 1], preferred_element_type=F32)

    def kv_put(s):
        for lo in range(0, rows, 128):
            r = slice(lo, lo + 128)
            for i in range(2):
                cols = slice(i * HD, (i + 1) * HD)
                kv_st[s, 0, i, r, :] = rope(ka_scr[r, cols], r, kg_ref).astype(BF16)
                kv_st[s, 1, i, r, :] = va_scr[r, cols].astype(BF16)

    def q_multiply(slot, lo, src):
        qa_scr[lo:lo + rows, :] = jnp.dot(src[...], w_scr[slot], preferred_element_type=F32)

    def q_put(slot, first):
        for lo in range(first, first + rows, 128):
            r = slice(lo, lo + 128)
            for i in range(bn // HD):
                t = rope(qa_scr[r, i * HD:(i + 1) * HD], r, qg_ref)
                length = jnp.sqrt(jnp.sum(t * t, axis=-1, keepdims=True))
                lane = lax.broadcasted_iota(jnp.int32, t.shape, 1)
                q_st[slot, i, r, :HD] = t.astype(BF16)
                q_st[slot, i, r, HD:] = jnp.where(lane == 0, length, 0.0).astype(BF16)

    def q_store(n, slot):
        return pltpu.make_async_copy(q_st.at[slot], q_out.at[pl.ds(n * (bn // HD), bn // HD)], q_sems.at[slot])

    my_rows = pl.ds(pl.multiple_of(chip * 2 * rows + core * rows, rows), rows)
    outs = (k_out, v_out)

    def local(s, i):
        return pltpu.make_async_copy(kv_st.at[s, i], outs[i].at[pl.ds(2 * s, 2), my_rows], loc_sems.at[s, i])

    def to_partner(s, i):
        return pltpu.make_async_remote_copy(
            src_ref=kv_st.at[s, i], dst_ref=outs[i].at[pl.ds(2 * (s - 2), 2), my_rows],
            send_sem=ps_sems.at[s - 2, i], recv_sem=pr_sems.at[s - 2, i],
            device_id={'sp': partner}, device_id_type=pl.DeviceIdType.MESH)

    def across(s, i):
        other = 2 + (core if s < 2 else 1 - core)
        return pltpu.make_async_remote_copy(
            src_ref=kv_st.at[s, i], dst_ref=outs[i].at[pl.ds(2 * (s % 2), 2), my_rows],
            send_sem=cs_sems.at[s, i], recv_sem=cr_sems.at[core, s % 2, i],
            device_id={'sp': other}, device_id_type=pl.DeviceIdType.MESH)

    def from_across(a, pair, i):
        r = pl.ds(a * rows, rows)
        return pltpu.make_async_remote_copy(
            src_ref=kv_st.at[0, i], dst_ref=outs[i].at[pl.ds(2 * pair, 2), r],
            send_sem=cs_sems.at[0, i], recv_sem=cr_sems.at[a, pair, i],
            device_id={'sp': a}, device_id_type=pl.DeviceIdType.MESH)

    def kv_ship(s):
        for i in range(2):
            (local if s < 2 else to_partner)(s, i).start()

        @pl.when(chip == 0)
        def _():
            for i in range(2):
                across(s, i).start()

    for i in range(4):
        x_load(i).start()
    k_weight(0, 0).start()
    v_weight(0, 1).start()
    barrier = pltpu.get_barrier_semaphore()
    for d in range(1, 4):
        pl.semaphore_signal(barrier, inc=1, device_id={'sp': (sp + d) % 4}, device_id_type=pl.DeviceIdType.MESH)
    pl.semaphore_wait(barrier, 3)
    for i in range(4):
        x_send(i).start()
    k_weight(1, 2).start()
    v_weight(1, 3).start()

    for i in range(4):
        x_load(i).wait()

    def norm_own(i, _):
        norm(own_scr, i)
        return 0

    lax.fori_loop(0, 4, norm_own, 0)
    k_weight(0, 0).wait()
    v_weight(0, 1).wait()
    kv_multiply(0)

    for s in range(1, 4):
        slot = 2 * (s % 2)
        k_weight(s, slot).wait()
        v_weight(s, slot + 1).wait()
        if s < 3:
            k_weight(s + 1, 2 - slot).start()
            v_weight(s + 1, 3 - slot).start()
        else:
            q_weight(0).start()
            q_weight(1).start()
        x_send(s - 1).wait_recv()
        kv_put(s - 1)
        norm(part_scr, s - 1)
        kv_multiply(slot)
        kv_ship(s - 1)

    q_weight(0).wait()
    q_weight(2).start()
    q_weight(3).start()
    x_send(3).wait_recv()
    kv_put(3)
    norm(part_scr, 3)
    q_multiply(0, 0, own_scr)
    q_multiply(0, rows, part_scr)
    kv_ship(3)

    def q_step(n, _):
        q_weight(n).wait()

        @pl.when(n + 3 < q_tiles)
        def _():
            q_weight(n + 3).start()

        slot = (n + 1) % 2

        @pl.when(n >= 3)
        def _():
            q_store(n - 3, slot).wait()

        q_put(slot, 0)
        q_multiply(n % 4, 0, own_scr)
        q_put(slot, rows)
        q_multiply(n % 4, rows, part_scr)
        q_store(n - 1, slot).start()
        return 0

    lax.fori_loop(1, q_tiles, q_step, 0)
    slot = (q_tiles - 1) % 2
    q_store(q_tiles - 3, slot).wait()
    q_put(slot, 0)
    q_put(slot, rows)
    q_store(q_tiles - 1, slot).start()

    for i in range(4):
        x_send(i).wait_send()
    for s in range(2):
        for i in range(2):
            local(s, i).wait()
            to_partner(s + 2, i).wait()

    @pl.when(chip == 0)
    def _():
        for s in range(4):
            for i in range(2):
                across(s, i).wait_send()

    @pl.when(chip == 1)
    def _():
        for a in range(2):
            for pair in range(2):
                for i in range(2):
                    from_across(a, pair, i).wait_recv()

    q_store(q_tiles - 2, 1 - slot).wait()
    q_store(q_tiles - 1, slot).wait()


def front(x, gain, w_q, w_k, w_v, cos, sin, q_gain, k_gain):
    rows, dim = x.shape
    bn = 256
    heads = w_q.shape[1] // HD // 2
    kv_heads = w_k.shape[1] // HD // 2
    vmem = pl.BlockSpec(memory_space=pltpu.VMEM)
    kv = jax.ShapeDtypeStruct((kv_heads, 4 * rows, HD), BF16)
    dma = pltpu.SemaphoreType.DMA
    return pl.pallas_call(
        front_kernel,
        in_specs=[ANY, vmem, ANY, ANY, ANY, vmem, vmem, vmem, vmem],
        out_specs=[ANY, ANY, ANY],
        out_shape=[jax.ShapeDtypeStruct((heads, 2 * rows, 2 * HD), BF16), kv, kv],
        scratch_shapes=[
            pltpu.VMEM((rows, dim), BF16),
            pltpu.VMEM((rows, dim), BF16),
            pltpu.VMEM((4, dim, bn), BF16),
            pltpu.VMEM((rows, bn), F32),
            pltpu.VMEM((rows, bn), F32),
            pltpu.VMEM((2 * rows, bn), F32),
            pltpu.VMEM((4, 2, 2, rows, HD), BF16),
            pltpu.VMEM((2, bn // HD, 2 * rows, 2 * HD), BF16),
            dma((4,)), dma((4,)), dma((4,)), dma((4,)), dma((2, 2)), dma((2, 2)), dma((2, 2)), dma((4, 2)), dma((2, 2, 2)), dma((2,)),
        ],
        compiler_params=pltpu.CompilerParams(vmem_limit_bytes=VMEM_LIMIT, collective_id=0, has_side_effects=True),
        cost_estimate=pl.CostEstimate(flops=2 * rows * dim * (w_q.shape[1] + 2 * w_k.shape[1]), bytes_accessed=dim * w_q.shape[1], transcendentals=0),
        name='front',
    )(x, gain.reshape(1, dim), w_q, w_k, w_v, cos, sin, q_gain.reshape(1, HD), k_gain.reshape(1, HD))


TILE = 128
KB = 512
SMALL = 2.0 ** -90


def attn_kernel(meta, q_ref, q_hbm, k_hbm, v_hbm, keep_ref, send_ref, k_scr, v_scr, o_scr, low_scr, qs_scr, s_scr, m_scr, sems, o_sems):
    g = pl.program_id(0)
    t = pl.program_id(1)
    tiles = pl.num_programs(1)
    chip = meta[0]
    core = meta[1]
    rows = k_hbm.shape[1] // 4
    group = q_ref.shape[0]
    seq = k_scr.shape[1]
    scale = HD ** -0.5 * math.log2(math.e)
    per = rows // TILE

    def base(tile):
        return (chip * 2 + jnp.where(tile < per, core, 1 - core)) * rows + tile % per * TILE

    @pl.when(jnp.logical_and(g == 0, t == 0))
    def _():
        for x in range(2):
            @pl.when(chip == x)
            def _():
                span = pl.ds(0, 2 * (x + 1) * rows)
                cps = [
                    pltpu.make_async_copy(src.at[:, span], dst.at[:, span, pl.ds(0, HD)], sems.at[i])
                    for i, (src, dst) in enumerate(((k_hbm, k_scr), (v_hbm, v_scr)))
                ]
                for cp in cps:
                    cp.start()
                if x == 0:
                    k_scr[:, 2 * rows:, :HD] = jnp.zeros((k_scr.shape[0], 2 * rows, HD), BF16)
                v_scr[:, :, HD:] = jnp.ones((v_scr.shape[0], seq, HD), BF16)
                for cp in cps:
                    cp.wait()

    @pl.when(t == 0)
    def _():
        k = k_scr[g, :, :HD]
        sums = jnp.dot(k * k, jnp.ones((HD, HD), BF16), preferred_element_type=F32)
        longest = jnp.sqrt(jnp.max(sums)) * 1.02
        lane = lax.broadcasted_iota(jnp.int32, (seq, HD), 1)
        k_scr[g, :, HD:] = jnp.where(lane == 0, -longest, 0.0).astype(BF16)
        low_scr[...] = jnp.ones_like(low_scr)

    pos0 = base(t)
    nfull = pos0 // KB
    off = pos0 - nfull * KB
    parts = 2
    hc = group // parts
    mc = hc * TILE

    it = g * tiles + t
    slot = it % 2

    def out_copy(ref, at_slot, at_tile, at_group):
        rows_at = pl.ds(pl.multiple_of((at_tile % per) * TILE, TILE), TILE)
        cols_at = pl.ds(pl.multiple_of(at_group * group * HD, group * HD), group * HD)
        return pltpu.make_async_copy(o_scr.at[at_slot], ref.at[rows_at, cols_at], o_sems.at[at_slot])

    def send_out(at_slot, at_tile):
        @pl.when(at_tile < per)
        def _():
            out_copy(keep_ref, at_slot, at_tile, g).start()

        @pl.when(at_tile >= per)
        def _():
            out_copy(send_ref, at_slot, at_tile, g).start()

    @pl.when(it >= 2)
    def _():
        out_copy(keep_ref, slot, 0, 0).wait()

    def run(blocks, width_last):
        total = blocks * KB + width_last
        for c in range(parts):
            q = q_ref[c * hc:(c + 1) * hc].reshape(mc, 2 * HD)
            ps = []
            for j in range(blocks + 1):
                width = KB if j < blocks else width_last
                s = lax.dot_general(q, k_scr[g, j * KB:j * KB + width, :], NT, preferred_element_type=F32)
                p = jnp.exp2(s * scale)
                if j == blocks:
                    row = lax.broadcasted_iota(jnp.int32, (hc, TILE, width), 1).reshape(mc, width) + off
                    col = lax.broadcasted_iota(jnp.int32, (mc, width), 1)
                    p = jnp.where(row >= col, p, 0.0)
                ps.append(p.astype(BF16))
            p = jnp.concatenate(ps, axis=1) if len(ps) > 1 else ps[0]
            acc = jnp.dot(p, v_scr[g, :total, :], preferred_element_type=F32)
            den = acc[:, HD:]
            o = (acc[:, :HD] * pltpu.reciprocal(den)).astype(BF16)
            for i in range(hc):
                h = c * hc + i
                o_scr[slot, :, h * HD:(h + 1) * HD] = o[i * TILE:(i + 1) * TILE]
            low_scr[...] = jnp.minimum(low_scr[...], jnp.min(den.reshape(mc // 8, 8, HD), axis=0))

    for blocks in range(seq // KB):
        for half in range(2):
            @pl.when(jnp.logical_and(nfull == blocks, off // 256 == half))
            def _():
                run(blocks, (half + 1) * 256)

    send_out(slot, t)

    def check():
        def redo(step, _):
            tile = step // group
            head = step % group
            cp = pltpu.make_async_copy(q_hbm.at[g * group + head, pl.ds(pl.multiple_of(tile * TILE, TILE), TILE)], qs_scr, sems.at[0])
            cp.start()
            cp.wait()
            q = qs_scr[:, :HD]
            pos = base(tile)
            last = pos // TILE
            row = lax.broadcasted_iota(jnp.int32, (TILE, TILE), 0)
            col = lax.broadcasted_iota(jnp.int32, (TILE, TILE), 1)
            m_scr[...] = jnp.full_like(m_scr, -jnp.inf)

            def first(j, _):
                k = k_scr[g, pl.ds(pl.multiple_of(j * TILE, TILE), TILE), :HD]
                s = lax.dot_general(q, k, NT, preferred_element_type=F32)
                s = jnp.where(row + pos >= col + j * TILE, s, -jnp.inf)
                s_scr[j] = s
                m_scr[...] = jnp.maximum(m_scr[...], s)
                return 0

            lax.fori_loop(0, last + 1, first, 0)
            m = jnp.max(m_scr[...], axis=1, keepdims=True)

            def second(j, acc):
                p = jnp.exp2((s_scr[j] - m) * scale).astype(BF16)
                v = v_scr[g, pl.ds(pl.multiple_of(j * TILE, TILE), TILE), :]
                return acc + jnp.dot(p, v, preferred_element_type=F32)

            acc = lax.fori_loop(0, last + 1, second, jnp.zeros((TILE, 2 * HD), F32))
            o = (acc[:, :HD] / acc[:, HD:]).astype(BF16)
            for h in range(group):
                @pl.when(head == h)
                def _():
                    o_scr[slot, :, h * HD:(h + 1) * HD] = o

            @pl.when(head == group - 1)
            def _():
                send_out(slot, tile)
                out_copy(keep_ref, slot, 0, 0).wait()

            return 0

        @pl.when(jnp.min(low_scr[...]) < SMALL)
        def _():
            out_copy(keep_ref, slot, 0, 0).wait()
            out_copy(keep_ref, 1 - slot, 0, 0).wait()
            lax.fori_loop(0, tiles * group, redo, 0)
            o_scr[1 - slot] = o_scr[slot]
            send_out(slot, t)
            send_out(1 - slot, t)

    @pl.when(t == tiles - 1)
    def _():
        check()

    @pl.when(it == tiles * pl.num_programs(0) - 1)
    def _():
        out_copy(keep_ref, slot, 0, 0).wait()
        out_copy(keep_ref, 1 - slot, 0, 0).wait()


def attention(chip, core, q, k, v):
    heads, q_rows, _ = q.shape
    rows = q_rows // 2
    seq = 4 * rows
    group = 8
    meta = jnp.stack([chip, core]).astype(jnp.int32)
    out = jax.ShapeDtypeStruct((rows, heads * HD), BF16)
    return pl.pallas_call(
        attn_kernel,
        grid_spec=pltpu.PrefetchScalarGridSpec(
            num_scalar_prefetch=1,
            grid=(heads // group, q_rows // TILE),
            in_specs=[pl.BlockSpec((group, TILE, 2 * HD), lambda g, t, m: (g, t, 0)), ANY, ANY, ANY],
            out_specs=[ANY, ANY],
            scratch_shapes=[
                pltpu.VMEM((heads // group, seq, 2 * HD), BF16),
                pltpu.VMEM((heads // group, seq, 2 * HD), BF16),
                pltpu.VMEM((2, TILE, group * HD), BF16),
                pltpu.VMEM((8, HD), F32),
                pltpu.VMEM((TILE, 2 * HD), BF16),
                pltpu.VMEM((seq // TILE, TILE, TILE), F32),
                pltpu.VMEM((TILE, TILE), F32),
                pltpu.SemaphoreType.DMA((2,)),
                pltpu.SemaphoreType.DMA((2,)),
            ],
        ),
        out_shape=[out, out],
        compiler_params=pltpu.CompilerParams(vmem_limit_bytes=VMEM_LIMIT),
        cost_estimate=pl.CostEstimate(flops=4 * heads * q_rows * seq * HD, bytes_accessed=6 * heads * q_rows * HD, transcendentals=0),
        name='attn',
    )(meta, q, q, k, v)


def out_kernel(meta, keep_ref, recv_ref, wa_ref, wb_ref, x_ref, o_ref):
    acc = jnp.dot(keep_ref[...], wa_ref[...], preferred_element_type=F32)
    acc += jnp.dot(recv_ref[...], wb_ref[...], preferred_element_type=F32)
    o_ref[...] = (acc + x_ref[...].astype(F32)).astype(BF16)


def out_project(core, keep, recv, w_o, x):
    rows, half = keep.shape
    dim = w_o.shape[1]
    bn = 256
    meta = jnp.stack([core]).astype(jnp.int32)
    full = pl.BlockSpec((rows, half), lambda n, m: (0, 0), pipeline_mode=pl.Buffered(1))
    tile = pl.BlockSpec((rows, bn), lambda n, m: (0, n))
    return pl.pallas_call(
        out_kernel,
        grid_spec=pltpu.PrefetchScalarGridSpec(
            num_scalar_prefetch=1,
            grid=(dim // bn,),
            in_specs=[full, full, pl.BlockSpec((half, bn), lambda n, m: (m[0], n)), pl.BlockSpec((half, bn), lambda n, m: (1 - m[0], n)), tile],
            out_specs=tile,
        ),
        out_shape=jax.ShapeDtypeStruct((rows, dim), BF16),
        compiler_params=pltpu.CompilerParams(vmem_limit_bytes=VMEM_LIMIT),
        cost_estimate=pl.CostEstimate(flops=4 * rows * half * dim, bytes_accessed=4 * half * dim, transcendentals=0),
        name='out_proj',
    )(meta, keep, recv, w_o, w_o, x)


PARTNER = [(0, 1), (1, 0), (2, 3), (3, 2)]


def solution(mesh):
    def device_step(hidden, ln_gain, w_q, w_k, w_v, w_o, q_gain, k_gain):
        rows = hidden.shape[0]
        sp = lax.axis_index('sp')
        chip = sp // 2
        core = sp % 2
        mine = jnp.arange(rows)
        positions = chip * 2 * rows + jnp.concatenate([core * rows + mine, (1 - core) * rows + mine])
        cos, sin = rope_tables(positions)
        q, k, v = front(hidden, ln_gain, w_q, w_k, w_v, cos, sin, q_gain, k_gain)
        keep, send = attention(chip, core, q, k, v)
        recv = lax.ppermute(send, 'sp', PARTNER)
        return out_project(core, keep, recv, w_o, hidden)

    row_spec = P(('dp', 'sp'), None)
    return jax.shard_map(device_step, mesh=mesh, in_specs=(row_spec, P(), P(), P(), P(), P(), P(), P()), out_specs=row_spec, check_vma=False)
```

profile of v0, /device:TPU:3, one launch (start us, length us, event | category | flops | bytes accessed | tf_op | source)
XLA Modules:
  0.0 217.3 jit_solution(13643699497693331154)
XLA Ops:
  0.0 1.3 reshape.29.g_ref
  1.4 1.9 fusion
  3.3 1.0 pad_maximum_fusion.cos_ref
  4.3 0.6 pad_add_fusion.meta
  4.9 1.0 pad_maximum_fusion.1.sin_ref
  5.9 72.4 %front.1 = (bf16[32,1024,256]{2,1,0:T(8,128)(2,1)}, bf16[4,2048,128]{2,1,0:T(8,128)(2,1)}, bf16[4,2048,128]{2,1,0:T(8,128)(2,1)}) custom-call(bf16[512,5120]{1,0:T(8,128)(2,1)} %x_ref.1, bf16[1,5120]{1,0:T(2,128)(2,1)} %reshape.29.g_ref, bf16[5120,8192]{1,0:T(8,128)(2,1)} %wq_hbm.1, bf16[5120,1024]{1,0:T(8,128)(2,1)} %wk_hbm.1, bf16[5120,1024]{1,0:T(8,128)(2,1)} %wv_hbm.1, ...), custom_call_target="tpu_custom_call" | custom-call | flops 53687091200 | bytes 41943040 | tf_op jit(solution)/shard_map/front/pallas_call | solution.py:257
  78.3 77.8 %attn.1 = (bf16[512,4096]{1,0:T(8,128)(2,1)}, bf16[512,4096]{1,0:T(8,128)(2,1)}) custom-call(s32[2]{0:T(128)} %pad_add_fusion.meta, bf16[32,1024,256]{2,1,0:T(8,128)(2,1)} %get-tuple-element.10.q_ref.q_hbm, bf16[32,1024,256]{2,1,0:T(8,128)(2,1)} %get-tuple-element.10.q_ref.q_hbm, bf16[4,2048,128]{2,1,0:T(8,128)(2,1)} %get-tuple-element.11.k_hbm, ...), custom_call_target="tpu_custom_call" | custom-call | flops 34359738368 | bytes 25165824 | tf_op jit(solution)/shard_map/attn/pallas_call | solution.py:455
  156.1 0.7 collective-permute-start
  156.8 6.8 %collective-permute-done.recv_ref = bf16[512,4096]{1,0:T(8,128)(2,1)} collective-permute-done((bf16[512,4096]{1,0:T(8,128)(2,1)}, bf16[512,4096]{1,0:T(8,128)(2,1)}, u32[]{:S(2)}, u32[]{:S(2)}) %collective-permute-start) | collective-permute-done | bytes 4194336 | tf_op jit(solution)/shard_map/ppermute | solution.py:523
  163.6 53.7 %out_proj.1 = bf16[512,5120]{1,0:T(8,128)(2,1)} custom-call(s32[1]{0:T(128)} %bitcast.meta, bf16[512,4096]{1,0:T(8,128)(2,1)} %get-tuple-element.13.keep_ref, bf16[512,4096]{1,0:T(8,128)(2,1)} %collective-permute-done.recv_ref, bf16[8192,5120]{1,0:T(8,128)(2,1)} %wb_ref.1, bf16[8192,5120]{1,0:T(8,128)(2,1)} %wb_ref.1, bf16[512,5120]{1,0:T(8,128)(2,1)} %x_ref.1), custom_call_target="tpu_custom_call" | custom-call | flops 42949672960 | bytes 83886080 | tf_op jit(solution)/shard_map/out_proj/pallas_call | solution.py:494
  (3 shorter events, 0.0 us)
Async XLA Ops:
  156.1 7.5 %collective-permute-start = (bf16[512,4096]{1,0:T(8,128)(2,1)}, bf16[512,4096]{1,0:T(8,128)(2,1)}, u32[]{:S(2)}, u32[]{:S(2)}) collective-permute-start(bf16[512,4096]{1,0:T(8,128)(2,1)} %get-tuple-element.14), channel_id=1, source_target_pairs={{0,1},{1,0},{2,3},{3,2},{4,5},{5,4},{6,7},{7,6}} | collective-permute-start | bytes 12582920 | tf_op jit(solution)/shard_map/ppermute | solution.py:523
where the time goes:
time: 218 us; the launch traced here: 217 us
  Pallas kernels  204 us (94%)
  waiting for transfers between devices  6.79 us (3%)
  other arithmetic  4.54 us (2%)
    pallas_call x1, Pallas kernels, attention(): pl.pallas_call(attn_kernel, grid_spec=pltpu.PrefetchScalarGridSpec(num_sc...  77.8 us
    pallas_call x1, Pallas kernels, front(): pl.pallas_call(front_kernel, in_specs=[ANY, vmem, ANY, ANY, ANY, vmem, vm...  72.4 us
    pallas_call x1, Pallas kernels, out_project(): pl.pallas_call(out_kernel, grid_spec=pltpu.PrefetchScalarGridSpec(num_sca...  53.7 us
    ppermute x1, waiting for transfers between devices, device_step(): recv = lax.ppermute(send, 'sp', PARTNER)  6.79 us
  transfers between devices with their start and end apart: 1, of which 1 were waited for; matrix products, arithmetic and copies ran while one was open for 0% of the time, Pallas kernels for 0%

commit v1 on v0

--- a/solution.py
+++ b/solution.py
@@ -3,6 +3,7 @@
 
 import jax
 import jax.numpy as jnp
+import numpy as np
 from jax import lax
 from jax.experimental import pallas as pl
 from jax.experimental.pallas import tpu as pltpu
@@ -18,17 +19,22 @@
 ANY = pl.BlockSpec(memory_space=pl.ANY)
 
 
-def rope_tables(positions):
+STRIDE = 64
+
+
+def rope_parts(seq):
     half = HD // 2
-    inv_freq = jnp.power(THETA, -(jnp.arange(half, dtype=F32) * (2.0 / HD)))
-    angles = positions.astype(F32)[:, None] * inv_freq[None, :]
-    cos = jnp.cos(angles)
-    sin = jnp.sin(angles)
-    return jnp.concatenate([cos, cos], axis=1), jnp.concatenate([-sin, sin], axis=1)
-
-
-def front_kernel(x_hbm, g_ref, wq_hbm, wk_hbm, wv_hbm, cos_ref, sin_ref, qg_ref, kg_ref, q_out, k_out, v_out,
-                 own_scr, part_scr, w_scr, ka_scr, va_scr, qa_scr, kv_st, q_st,
+    inv_freq = THETA ** -(np.arange(half) * (2.0 / HD))
+    parts = []
+    for positions in (np.arange(0, seq, STRIDE), np.arange(STRIDE)):
+        angles = positions[:, None] * inv_freq[None, :]
+        parts.append(np.concatenate([np.cos(angles), np.cos(angles)], axis=1))
+        parts.append(np.concatenate([-np.sin(angles), np.sin(angles)], axis=1))
+    return np.concatenate(parts, axis=0).astype(np.float32)
+
+
+def front_kernel(x_hbm, gain_ref, wq_hbm, wk_hbm, wv_hbm, tab_ref, qgain_ref, kgain_ref, q_out, k_out, v_out,
+                 g_ref, qg_ref, kg_ref, cos_ref, sin_ref, own_scr, part_scr, w_scr, ka_scr, va_scr, qa_scr, kv_st, q_st,
                  x_sems, w_sems, xs_sems, xr_sems, loc_sems, ps_sems, pr_sems, cs_sems, cr_sems, q_sems):
     sp = lax.axis_index('sp')
     chip = sp // 2
@@ -74,11 +80,11 @@
             inv = lax.rsqrt(jnp.sum(total, axis=1, keepdims=True) * (1.0 / dim) + EPS)
             for lo in range(0, dim, width):
                 x = ref[r, lo:lo + width].astype(F32)
-                ref[r, lo:lo + width] = (x * inv * g_ref[:, lo:lo + width].astype(F32)).astype(BF16)
-
-    def rope(acc, at, gain_ref):
+                ref[r, lo:lo + width] = (x * inv * g_ref[:, lo:lo + width]).astype(BF16)
+
+    def rope(acc, at, gain):
         var = jnp.mean(acc * acc, axis=-1, keepdims=True)
-        t = acc * lax.rsqrt(var + EPS) * gain_ref[...].astype(F32)
+        t = acc * lax.rsqrt(var + EPS) * gain[...]
         return t * cos_ref[at, :] + pltpu.roll(t, HD // 2, 1) * sin_ref[at, :]
 
     def kv_multiply(slot):
@@ -156,6 +162,21 @@
         x_send(i).start()
     k_weight(1, 2).start()
     v_weight(1, 3).start()
+
+    g_ref[...] = gain_ref[...].astype(F32).reshape(1, dim)
+    qg_ref[...] = qgain_ref[...].astype(F32).reshape(1, HD)
+    kg_ref[...] = kgain_ref[...].astype(F32).reshape(1, HD)
+    coarse = 4 * rows // STRIDE
+    cos_b = tab_ref[2 * coarse:2 * coarse + STRIDE, :]
+    sin_b = tab_ref[2 * coarse + STRIDE:, :]
+    for j in range(2 * rows // STRIDE):
+        side = core if j * STRIDE < rows else 1 - core
+        a = (chip * 2 + side) * (rows // STRIDE) + j % (rows // STRIDE)
+        cos_a = tab_ref[pl.ds(a, 1), :]
+        sin_a = tab_ref[pl.ds(coarse + a, 1), :]
+        r = slice(j * STRIDE, (j + 1) * STRIDE)
+        cos_ref[r, :] = cos_a * cos_b - sin_a * sin_b
+        sin_ref[r, :] = sin_a * cos_b + cos_a * sin_b
 
     for i in range(4):
         x_load(i).wait()
@@ -246,7 +267,7 @@
     q_store(q_tiles - 1, slot).wait()
 
 
-def front(x, gain, w_q, w_k, w_v, cos, sin, q_gain, k_gain):
+def front(x, gain, w_q, w_k, w_v, q_gain, k_gain):
     rows, dim = x.shape
     bn = 256
     heads = w_q.shape[1] // HD // 2
@@ -256,10 +277,15 @@
     dma = pltpu.SemaphoreType.DMA
     return pl.pallas_call(
         front_kernel,
-        in_specs=[ANY, vmem, ANY, ANY, ANY, vmem, vmem, vmem, vmem],
+        in_specs=[ANY, vmem, ANY, ANY, ANY, vmem, vmem, vmem],
         out_specs=[ANY, ANY, ANY],
         out_shape=[jax.ShapeDtypeStruct((heads, 2 * rows, 2 * HD), BF16), kv, kv],
         scratch_shapes=[
+            pltpu.VMEM((1, dim), F32),
+            pltpu.VMEM((1, HD), F32),
+            pltpu.VMEM((1, HD), F32),
+            pltpu.VMEM((2 * rows, HD), F32),
+            pltpu.VMEM((2 * rows, HD), F32),
             pltpu.VMEM((rows, dim), BF16),
             pltpu.VMEM((rows, dim), BF16),
             pltpu.VMEM((4, dim, bn), BF16),
@@ -273,7 +299,7 @@
         compiler_params=pltpu.CompilerParams(vmem_limit_bytes=VMEM_LIMIT, collective_id=0, has_side_effects=True),
         cost_estimate=pl.CostEstimate(flops=2 * rows * dim * (w_q.shape[1] + 2 * w_k.shape[1]), bytes_accessed=dim * w_q.shape[1], transcendentals=0),
         name='front',
-    )(x, gain.reshape(1, dim), w_q, w_k, w_v, cos, sin, q_gain.reshape(1, HD), k_gain.reshape(1, HD))
+    )(x, gain, w_q, w_k, w_v, jnp.asarray(rope_parts(4 * rows)), q_gain, k_gain)
 
 
 TILE = 128
@@ -281,80 +307,90 @@
 SMALL = 2.0 ** -90
 
 
-def attn_kernel(meta, q_ref, q_hbm, k_hbm, v_hbm, keep_ref, send_ref, k_scr, v_scr, o_scr, low_scr, qs_scr, s_scr, m_scr, sems, o_sems):
-    g = pl.program_id(0)
-    t = pl.program_id(1)
-    tiles = pl.num_programs(1)
-    chip = meta[0]
-    core = meta[1]
-    rows = k_hbm.shape[1] // 4
-    group = q_ref.shape[0]
-    seq = k_scr.shape[1]
+def attn_kernel(q_hbm, k_hbm, v_hbm, keep_ref, send_ref, q_scr, k_scr, v_scr, o_scr, low_scr, s_scr, m_scr, q_sems, k_sems, v_sems, o_sems):
+    sp = lax.axis_index('sp')
+    chip = sp // 2
+    core = sp % 2
+    groups, seq, _ = k_hbm.shape
+    rows = seq // 4
+    group = q_scr.shape[0] // groups
+    tiles = 2 * rows // TILE
+    per = rows // TILE
     scale = HD ** -0.5 * math.log2(math.e)
-    per = rows // TILE
 
     def base(tile):
         return (chip * 2 + jnp.where(tile < per, core, 1 - core)) * rows + tile % per * TILE
 
-    @pl.when(jnp.logical_and(g == 0, t == 0))
-    def _():
+    def kv_load(g, x):
+        span = pl.ds(0, 2 * (x + 1) * rows)
+        return [
+            pltpu.make_async_copy(src.at[g, span], dst.at[g, span, pl.ds(0, HD)], sems.at[g])
+            for src, dst, sems in ((k_hbm, k_scr, k_sems), (v_hbm, v_scr, v_sems))
+        ]
+
+    def q_load(t):
+        r = pl.ds(t * TILE, TILE)
+        return pltpu.make_async_copy(q_hbm.at[:, r], q_scr.at[:, r], q_sems.at[t])
+
+    def kv_start(g):
         for x in range(2):
             @pl.when(chip == x)
             def _():
-                span = pl.ds(0, 2 * (x + 1) * rows)
-                cps = [
-                    pltpu.make_async_copy(src.at[:, span], dst.at[:, span, pl.ds(0, HD)], sems.at[i])
-                    for i, (src, dst) in enumerate(((k_hbm, k_scr), (v_hbm, v_scr)))
-                ]
-                for cp in cps:
+                for cp in kv_load(g, x):
                     cp.start()
-                if x == 0:
-                    k_scr[:, 2 * rows:, :HD] = jnp.zeros((k_scr.shape[0], 2 * rows, HD), BF16)
-                v_scr[:, :, HD:] = jnp.ones((v_scr.shape[0], seq, HD), BF16)
-                for cp in cps:
+
+    def kv_wait(g):
+        for x in range(2):
+            @pl.when(chip == x)
+            def _():
+                for cp in kv_load(g, x):
                     cp.wait()
 
-    @pl.when(t == 0)
+    kv_start(0)
+    q_load(0).start()
+    for g in range(1, groups):
+        kv_start(g)
+    for t in range(1, tiles):
+        q_load(t).start()
+
+    @pl.when(chip == 0)
     def _():
+        k_scr[:, 2 * rows:, :HD] = jnp.zeros((groups, 2 * rows, HD), BF16)
+
+    v_scr[:, :, HD:] = jnp.ones((groups, seq, HD), BF16)
+
+    def open_group(g):
+        kv_wait(g)
         k = k_scr[g, :, :HD]
         sums = jnp.dot(k * k, jnp.ones((HD, HD), BF16), preferred_element_type=F32)
         longest = jnp.sqrt(jnp.max(sums)) * 1.02
         lane = lax.broadcasted_iota(jnp.int32, (seq, HD), 1)
         k_scr[g, :, HD:] = jnp.where(lane == 0, -longest, 0.0).astype(BF16)
-        low_scr[...] = jnp.ones_like(low_scr)
-
-    pos0 = base(t)
-    nfull = pos0 // KB
-    off = pos0 - nfull * KB
+        low_scr[g] = jnp.ones((8, HD), F32)
+
+    def out_copy(ref, slot, tile, g):
+        rows_at = pl.ds(pl.multiple_of((tile % per) * TILE, TILE), TILE)
+        cols_at = pl.ds(pl.multiple_of(g * group * HD, group * HD), group * HD)
+        return pltpu.make_async_copy(o_scr.at[slot], ref.at[rows_at, cols_at], o_sems.at[slot])
+
+    def send_out(slot, tile, g):
+        @pl.when(tile < per)
+        def _():
+            out_copy(keep_ref, slot, tile, g).start()
+
+        @pl.when(tile >= per)
+        def _():
+            out_copy(send_ref, slot, tile, g).start()
+
     parts = 2
     hc = group // parts
     mc = hc * TILE
 
-    it = g * tiles + t
-    slot = it % 2
-
-    def out_copy(ref, at_slot, at_tile, at_group):
-        rows_at = pl.ds(pl.multiple_of((at_tile % per) * TILE, TILE), TILE)
-        cols_at = pl.ds(pl.multiple_of(at_group * group * HD, group * HD), group * HD)
-        return pltpu.make_async_copy(o_scr.at[at_slot], ref.at[rows_at, cols_at], o_sems.at[at_slot])
-
-    def send_out(at_slot, at_tile):
-        @pl.when(at_tile < per)
-        def _():
-            out_copy(keep_ref, at_slot, at_tile, g).start()
-
-        @pl.when(at_tile >= per)
-        def _():
-            out_copy(send_ref, at_slot, at_tile, g).start()
-
-    @pl.when(it >= 2)
-    def _():
-        out_copy(keep_ref, slot, 0, 0).wait()
-
-    def run(blocks, width_last):
+    def run(g, t, slot, off, blocks, width_last):
         total = blocks * KB + width_last
+        at = pl.ds(pl.multiple_of(t * TILE, TILE), TILE)
         for c in range(parts):
-            q = q_ref[c * hc:(c + 1) * hc].reshape(mc, 2 * HD)
+            q = q_scr[pl.ds(g * group + c * hc, hc), at, :].reshape(mc, 2 * HD)
             ps = []
             for j in range(blocks + 1):
                 width = KB if j < blocks else width_last
@@ -372,24 +408,13 @@
             for i in range(hc):
                 h = c * hc + i
                 o_scr[slot, :, h * HD:(h + 1) * HD] = o[i * TILE:(i + 1) * TILE]
-            low_scr[...] = jnp.minimum(low_scr[...], jnp.min(den.reshape(mc // 8, 8, HD), axis=0))
-
-    for blocks in range(seq // KB):
-        for half in range(2):
-            @pl.when(jnp.logical_and(nfull == blocks, off // 256 == half))
-            def _():
-                run(blocks, (half + 1) * 256)
-
-    send_out(slot, t)
-
-    def check():
-        def redo(step, _):
+            low_scr[g] = jnp.minimum(low_scr[g], jnp.min(den.reshape(mc // 8, 8, HD), axis=0))
+
+    def redo(g, slot):
+        def one(step, _):
             tile = step // group
             head = step % group
-            cp = pltpu.make_async_copy(q_hbm.at[g * group + head, pl.ds(pl.multiple_of(tile * TILE, TILE), TILE)], qs_scr, sems.at[0])
-            cp.start()
-            cp.wait()
-            q = qs_scr[:, :HD]
+            q = q_scr[g * group + head, pl.ds(pl.multiple_of(tile * TILE, TILE), TILE), :HD]
             pos = base(tile)
             last = pos // TILE
             row = lax.broadcasted_iota(jnp.int32, (TILE, TILE), 0)
@@ -421,107 +446,211 @@
 
             @pl.when(head == group - 1)
             def _():
-                send_out(slot, tile)
+                send_out(slot, tile, g)
                 out_copy(keep_ref, slot, 0, 0).wait()
 
             return 0
 
-        @pl.when(jnp.min(low_scr[...]) < SMALL)
+        lax.fori_loop(0, tiles * group, one, 0)
+
+    def step(it, _):
+        t = it // groups
+        g = it % groups
+        slot = it % 2
+
+        @pl.when(g == 0)
+        def _():
+            q_load(t).wait()
+
+        @pl.when(t == 0)
+        def _():
+            open_group(g)
+
+        @pl.when(it >= 2)
         def _():
             out_copy(keep_ref, slot, 0, 0).wait()
-            out_copy(keep_ref, 1 - slot, 0, 0).wait()
-            lax.fori_loop(0, tiles * group, redo, 0)
-            o_scr[1 - slot] = o_scr[slot]
-            send_out(slot, t)
-            send_out(1 - slot, t)
-
-    @pl.when(t == tiles - 1)
+
+        pos0 = base(t)
+        nfull = pos0 // KB
+        off = pos0 - nfull * KB
+        for blocks in range(seq // KB):
+            for half in range(2):
+                @pl.when(jnp.logical_and(nfull == blocks, off // 256 == half))
+                def _():
+                    run(g, t, slot, off, blocks, (half + 1) * 256)
+
+        send_out(slot, t, g)
+        return 0
+
+    lax.fori_loop(0, groups * tiles, step, 0)
+    for slot in range(2):
+        out_copy(keep_ref, slot, 0, 0).wait()
+
+    @pl.when(jnp.min(low_scr[...]) < SMALL)
     def _():
-        check()
-
-    @pl.when(it == tiles * pl.num_programs(0) - 1)
-    def _():
-        out_copy(keep_ref, slot, 0, 0).wait()
-        out_copy(keep_ref, 1 - slot, 0, 0).wait()
-
-
-def attention(chip, core, q, k, v):
+        def group_again(g, _):
+            redo(g, 0)
+            return 0
+
+        lax.fori_loop(0, groups, group_again, 0)
+
+
+def attention(q, k, v):
     heads, q_rows, _ = q.shape
-    rows = q_rows // 2
-    seq = 4 * rows
-    group = 8
-    meta = jnp.stack([chip, core]).astype(jnp.int32)
-    out = jax.ShapeDtypeStruct((rows, heads * HD), BF16)
+    groups, seq, _ = k.shape
+    group = heads // groups
+    out = jax.ShapeDtypeStruct((q_rows // 2, heads * HD), BF16)
+    dma = pltpu.SemaphoreType.DMA
     return pl.pallas_call(
         attn_kernel,
-        grid_spec=pltpu.PrefetchScalarGridSpec(
-            num_scalar_prefetch=1,
-            grid=(heads // group, q_rows // TILE),
-            in_specs=[pl.BlockSpec((group, TILE, 2 * HD), lambda g, t, m: (g, t, 0)), ANY, ANY, ANY],
-            out_specs=[ANY, ANY],
-            scratch_shapes=[
-                pltpu.VMEM((heads // group, seq, 2 * HD), BF16),
-                pltpu.VMEM((heads // group, seq, 2 * HD), BF16),
-                pltpu.VMEM((2, TILE, group * HD), BF16),
-                pltpu.VMEM((8, HD), F32),
-                pltpu.VMEM((TILE, 2 * HD), BF16),
-                pltpu.VMEM((seq // TILE, TILE, TILE), F32),
-                pltpu.VMEM((TILE, TILE), F32),
-                pltpu.SemaphoreType.DMA((2,)),
-                pltpu.SemaphoreType.DMA((2,)),
-            ],
-        ),
+        in_specs=[ANY, ANY, ANY],
+        out_specs=[ANY, ANY],
+        scratch_shapes=[
+            pltpu.VMEM((heads, q_rows, 2 * HD), BF16),
+            pltpu.VMEM((groups, seq, 2 * HD), BF16),
+            pltpu.VMEM((groups, seq, 2 * HD), BF16),
+            pltpu.VMEM((2, TILE, group * HD), BF16),
+            pltpu.VMEM((groups, 8, HD), F32),
+            pltpu.VMEM((seq // TILE, TILE, TILE), F32),
+            pltpu.VMEM((TILE, TILE), F32),
+            dma((q_rows // TILE,)), dma((groups,)), dma((groups,)), dma((2,)),
+        ],
         out_shape=[out, out],
         compiler_params=pltpu.CompilerParams(vmem_limit_bytes=VMEM_LIMIT),
         cost_estimate=pl.CostEstimate(flops=4 * heads * q_rows * seq * HD, bytes_accessed=6 * heads * q_rows * HD, transcendentals=0),
         name='attn',
-    )(meta, q, q, k, v)
-
-
-def out_kernel(meta, keep_ref, recv_ref, wa_ref, wb_ref, x_ref, o_ref):
-    acc = jnp.dot(keep_ref[...], wa_ref[...], preferred_element_type=F32)
-    acc += jnp.dot(recv_ref[...], wb_ref[...], preferred_element_type=F32)
-    o_ref[...] = (acc + x_ref[...].astype(F32)).astype(BF16)
-
-
-def out_project(core, keep, recv, w_o, x):
+    )(q, k, v)
+
+
+def out_kernel(keep_hbm, send_hbm, wo_hbm, x_hbm, out_hbm, keep_scr, recv_scr, x_scr, w_scr, acc_scr, o_st,
+               in_sems, x_sem, w_sems, s_sems, r_sems, o_sems):
+    sp = lax.axis_index('sp')
+    chip = sp // 2
+    core = sp % 2
+    partner = chip * 2 + 1 - core
+    rows, half = keep_hbm.shape
+    bn = w_scr.shape[2]
+    tiles = wo_hbm.shape[1] // bn
+    slots = w_scr.shape[0]
+    pieces = 4
+    piece = half // pieces
+
+    def keep_load(i):
+        cols = pl.ds(i * piece, piece)
+        return pltpu.make_async_copy(keep_hbm.at[:, cols], keep_scr.at[:, cols], in_sems.at[i])
+
+    def exchange(i):
+        cols = pl.ds(i * piece, piece)
+        return pltpu.make_async_remote_copy(
+            src_ref=send_hbm.at[:, cols], dst_ref=recv_scr.at[:, cols], send_sem=s_sems.at[i], recv_sem=r_sems.at[i],
+            device_id={'sp': partner}, device_id_type=pl.DeviceIdType.MESH)
+
+    def weight(i):
+        side = jnp.where(i < tiles, core, 1 - core)
+        r = pl.ds(pl.multiple_of(side * half, half), half)
+        c = pl.ds(pl.multiple_of(i % tiles * bn, bn), bn)
+        return pltpu.make_async_copy(wo_hbm.at[r, c], w_scr.at[i % slots], w_sems.at[i % slots])
+
+    def first_weight(i):
+        r = pl.ds(pl.multiple_of(core * half + i * piece, piece), piece)
+        return pltpu.make_async_copy(wo_hbm.at[r, pl.ds(0, bn)], w_scr.at[0, pl.ds(i * piece, piece)], in_sems.at[pieces + i])
+
+    x_load = pltpu.make_async_copy(x_hbm, x_scr, x_sem)
+
+    for i in range(pieces):
+        keep_load(i).start()
+        first_weight(i).start()
+    barrier = pltpu.get_barrier_semaphore()
+    pl.semaphore_signal(barrier, inc=1, device_id={'sp': partner}, device_id_type=pl.DeviceIdType.MESH)
+    pl.semaphore_wait(barrier, 1)
+    for i in range(pieces):
+        exchange(i).start()
+    for i in range(1, slots - 1):
+        weight(i).start()
+    x_load.start()
+
+    for i in range(pieces):
+        keep_load(i).wait()
+        first_weight(i).wait()
+        k = slice(i * piece, (i + 1) * piece)
+        part = jnp.dot(keep_scr[:, k], w_scr[0, k, :], preferred_element_type=F32)
+        acc_scr[0] = part if i == 0 else acc_scr[0] + part
+    weight(slots - 1).start()
+
+    def own_half(n, _):
+        weight(n).wait()
+        weight(n + slots - 1).start()
+        acc_scr[n] = jnp.dot(keep_scr[...], w_scr[n % slots], preferred_element_type=F32)
+        return 0
+
+    lax.fori_loop(1, tiles, own_half, 0)
+    x_load.wait()
+    for i in range(pieces):
+        exchange(i).wait_recv()
+
+    def store(n, slot):
+        return pltpu.make_async_copy(o_st.at[slot], out_hbm.at[:, pl.ds(pl.multiple_of(n * bn, bn), bn)], o_sems.at[slot])
+
+    def other_half(n, _):
+        i = n + tiles
+        weight(i).wait()
+
+        @pl.when(i + slots - 1 < 2 * tiles)
+        def _():
+            weight(i + slots - 1).start()
+
+        slot = n % 2
+
+        @pl.when(n >= 2)
+        def _():
+            store(n - 2, slot).wait()
+
+        cols = pl.ds(pl.multiple_of(n * bn, bn), bn)
+        for lo in range(0, rows, rows // 2):
+            r = slice(lo, lo + rows // 2)
+            total = acc_scr[n, r, :] + jnp.dot(recv_scr[r, :], w_scr[i % slots], preferred_element_type=F32)
+            o_st[slot, r, :] = (total + x_scr[r, cols].astype(F32)).astype(BF16)
+        store(n, slot).start()
+        return 0
+
+    lax.fori_loop(0, tiles, other_half, 0)
+    for n in range(tiles - 2, tiles):
+        store(n, n % 2).wait()
+    for i in range(pieces):
+        exchange(i).wait_send()
+
+
+def out_project(keep, send, w_o, x):
     rows, half = keep.shape
     dim = w_o.shape[1]
-    bn = 256
-    meta = jnp.stack([core]).astype(jnp.int32)
-    full = pl.BlockSpec((rows, half), lambda n, m: (0, 0), pipeline_mode=pl.Buffered(1))
-    tile = pl.BlockSpec((rows, bn), lambda n, m: (0, n))
+    bn = 512
+    slots = 4
+    dma = pltpu.SemaphoreType.DMA
     return pl.pallas_call(
         out_kernel,
-        grid_spec=pltpu.PrefetchScalarGridSpec(
-            num_scalar_prefetch=1,
-            grid=(dim // bn,),
-            in_specs=[full, full, pl.BlockSpec((half, bn), lambda n, m: (m[0], n)), pl.BlockSpec((half, bn), lambda n, m: (1 - m[0], n)), tile],
-            out_specs=tile,
-        ),
+        in_specs=[ANY, ANY, ANY, ANY],
+        out_specs=ANY,
+        scratch_shapes=[
+            pltpu.VMEM((rows, half), BF16),
+            pltpu.VMEM((rows, half), BF16),
+            pltpu.VMEM((rows, dim), BF16),
+            pltpu.VMEM((slots, half, bn), BF16),
+            pltpu.VMEM((dim // bn, rows, bn), F32),
+            pltpu.VMEM((2, rows, bn), BF16),
+            dma((8,)), dma, dma((slots,)), dma((4,)), dma((4,)), dma((2,)),
+        ],
         out_shape=jax.ShapeDtypeStruct((rows, dim), BF16),
-        compiler_params=pltpu.CompilerParams(vmem_limit_bytes=VMEM_LIMIT),
+        compiler_params=pltpu.CompilerParams(vmem_limit_bytes=VMEM_LIMIT, collective_id=1, has_side_effects=True),
         cost_estimate=pl.CostEstimate(flops=4 * rows * half * dim, bytes_accessed=4 * half * dim, transcendentals=0),
         name='out_proj',
-    )(meta, keep, recv, w_o, w_o, x)
-
-
-PARTNER = [(0, 1), (1, 0), (2, 3), (3, 2)]
+    )(keep, send, w_o, x)
 
 
 def solution(mesh):
     def device_step(hidden, ln_gain, w_q, w_k, w_v, w_o, q_gain, k_gain):
-        rows = hidden.shape[0]
-        sp = lax.axis_index('sp')
-        chip = sp // 2
-        core = sp % 2
-        mine = jnp.arange(rows)
-        positions = chip * 2 * rows + jnp.concatenate([core * rows + mine, (1 - core) * rows + mine])
-        cos, sin = rope_tables(positions)
-        q, k, v = front(hidden, ln_gain, w_q, w_k, w_v, cos, sin, q_gain, k_gain)
-        keep, send = attention(chip, core, q, k, v)
-        recv = lax.ppermute(send, 'sp', PARTNER)
-        return out_project(core, keep, recv, w_o, hidden)
+        q, k, v = front(hidden, ln_gain, w_q, w_k, w_v, q_gain, k_gain)
+        keep, send = attention(q, k, v)
+        return out_project(keep, send, w_o, hidden)
 
     row_spec = P(('dp', 'sp'), None)
     return jax.shard_map(device_step, mesh=mesh, in_specs=(row_spec, P(), P(), P(), P(), P(), P(), P()), out_specs=row_spec, check_vma=False)

time: 218 us -> 203 us (0.931)
  waiting for transfers between devices: 6.79 us -> 0 us
  Pallas kernels: 204 us -> 198 us
  other arithmetic: 4.54 us -> 0 us
  local copies, waits for them, and re-layouts: 1.32 us -> 5.18 us
    ppermute x1 -> x0, waiting for transfers between devices: 6.79 us -> none  [device_step(): recv = lax.ppermute(send, 'sp', PARTNER)]
    pallas_call x2, Pallas kernels: 132 us -> 126 us  [the longest x1 75.1 us: attention(): pl.pallas_call(attn_kernel, in_specs=[ANY, ANY, ANY], out_specs=[ANY, ANY...]
    unnamed x0 -> x1, local copies, waits for them, and re-layouts: none -> 5.18 us
  transfers between devices with their start and end apart: 1 -> 0, of which waited for: 1 -> 0; matrix products, arithmetic and copies ran while one was open for 0% -> 0% of each run, Pallas kernels for 0% -> 0%
where the time goes in v1:
time: 203 us
  Pallas kernels  198 us (98%)
  local copies, waits for them, and re-layouts  5.18 us (3%)
    pallas_call x1, Pallas kernels, attention(): pl.pallas_call(attn_kernel, in_specs=[ANY, ANY, ANY], out_specs=[ANY, ANY...  75.1 us
    pallas_call x1, Pallas kernels, front(): pl.pallas_call(front_kernel, in_specs=[ANY, vmem, ANY, ANY, ANY, vmem, vm...  72.2 us
    pallas_call x1, Pallas kernels, out_project(): pl.pallas_call(out_kernel, in_specs=[ANY, ANY, ANY, ANY], out_specs=ANY,...  50.5 us
    unnamed x1, local copies, waits for them, and re-layouts  5.18 us

profile of v1, /device:TPU:3, one launch (start us, length us, event | category | flops | bytes accessed | tf_op | source)
XLA Modules:
  0.0 203.0 jit_solution(6504975260008594499)
XLA Ops:
  0.0 72.2 %front.1 = (bf16[32,1024,256]{2,1,0:T(8,128)(2,1)}, bf16[4,2048,128]{2,1,0:T(8,128)(2,1)}, bf16[4,2048,128]{2,1,0:T(8,128)(2,1)}) custom-call(bf16[512,5120]{1,0:T(8,128)(2,1)} %x_hbm.3, bf16[5120]{0:T(1024)(128)(2,1)} %gain_ref.1, bf16[5120,8192]{1,0:T(8,128)(2,1)} %wq_hbm.1, bf16[5120,1024]{1,0:T(8,128)(2,1)} %wk_hbm.1, bf16[5120,1024]{1,0:T(8,128)(2,1)} %wv_hbm.1, ...), custom_call_target="tpu_custom_call" | custom-call | flops 53687091200 | bytes 41943040 | tf_op jit(solution)/shard_map/front/pallas_call | solution.py:278
  72.2 75.1 %attn.1 = (bf16[512,4096]{1,0:T(8,128)(2,1)}, bf16[512,4096]{1,0:T(8,128)(2,1)}) custom-call(bf16[32,1024,256]{2,1,0:T(8,128)(2,1)} %get-tuple-element.10.q_hbm, bf16[4,2048,128]{2,1,0:T(8,128)(2,1)} %get-tuple-element.11.k_hbm, bf16[4,2048,128]{2,1,0:T(8,128)(2,1)} %get-tuple-element.12.v_hbm), custom_call_target="tpu_custom_call" | custom-call | flops 34359738368 | bytes 25165824 | tf_op jit(solution)/shard_map/attn/pallas_call | solution.py:504
  147.4 50.5 %out_proj.1 = bf16[512,5120]{1,0:T(8,128)(2,1)} custom-call(bf16[512,4096]{1,0:T(8,128)(2,1)} %get-tuple-element.13.keep_hbm, bf16[512,4096]{1,0:T(8,128)(2,1)} %get-tuple-element.14.send_hbm, bf16[8192,5120]{1,0:T(8,128)(2,1)} %wo_hbm.1, bf16[512,5120]{1,0:T(8,128)(2,1)} %x_hbm.3), custom_call_target="tpu_custom_call" | custom-call | flops 42949672960 | bytes 83886080 | tf_op jit(solution)/shard_map/out_proj/pallas_call | solution.py:629
  197.9 5.2 %copy.11 = bf16[512,5120]{1,0:T(8,128)(2,1)} copy(bf16[512,5120]{1,0:T(8,128)(2,1)} %out_proj.1) | data formatting | bytes 10485760

commit v2 on v1

--- a/solution.py
+++ b/solution.py
@@ -87,9 +87,10 @@
         t = acc * lax.rsqrt(var + EPS) * gain[...]
         return t * cos_ref[at, :] + pltpu.roll(t, HD // 2, 1) * sin_ref[at, :]
 
-    def kv_multiply(slot):
-        ka_scr[...] = jnp.dot(own_scr[...], w_scr[slot], preferred_element_type=F32)
-        va_scr[...] = jnp.dot(own_scr[...], w_scr[slot + 1], preferred_element_type=F32)
+    def kv_multiply(slot, lo, n):
+        r = slice(lo, lo + n)
+        ka_scr[r, :] = jnp.dot(own_scr[r, :], w_scr[slot], preferred_element_type=F32)
+        va_scr[r, :] = jnp.dot(own_scr[r, :], w_scr[slot + 1], preferred_element_type=F32)
 
     def kv_put(s):
         for lo in range(0, rows, 128):
@@ -128,7 +129,7 @@
             device_id={'sp': partner}, device_id_type=pl.DeviceIdType.MESH)
 
     def across(s, i):
-        other = 2 + (core if s < 2 else 1 - core)
+        other = 2 + jnp.where(s < 2, core, 1 - core)
         return pltpu.make_async_remote_copy(
             src_ref=kv_st.at[s, i], dst_ref=outs[i].at[pl.ds(2 * (s % 2), 2), my_rows],
             send_sem=cs_sems.at[s, i], recv_sem=cr_sems.at[core, s % 2, i],
@@ -143,7 +144,13 @@
 
     def kv_ship(s):
         for i in range(2):
-            (local if s < 2 else to_partner)(s, i).start()
+            @pl.when(s < 2)
+            def _():
+                local(s, i).start()
+
+            @pl.when(s >= 2)
+            def _():
+                to_partner(s, i).start()
 
         @pl.when(chip == 0)
         def _():
@@ -185,26 +192,37 @@
         norm(own_scr, i)
         return 0
 
-    lax.fori_loop(0, 4, norm_own, 0)
+    lax.fori_loop(0, 2, norm_own, 0)
     k_weight(0, 0).wait()
     v_weight(0, 1).wait()
-    kv_multiply(0)
-
-    for s in range(1, 4):
+    norm(own_scr, 2)
+    norm(own_scr, 3)
+    kv_multiply(0, 0, rows // 2)
+    kv_multiply(0, rows // 2, rows // 2)
+
+    def kv_step(s, _):
         slot = 2 * (s % 2)
         k_weight(s, slot).wait()
         v_weight(s, slot + 1).wait()
-        if s < 3:
+
+        @pl.when(s < 3)
+        def _():
             k_weight(s + 1, 2 - slot).start()
             v_weight(s + 1, 3 - slot).start()
-        else:
+
+        @pl.when(s == 3)
+        def _():
             q_weight(0).start()
             q_weight(1).start()
+
         x_send(s - 1).wait_recv()
         kv_put(s - 1)
         norm(part_scr, s - 1)
-        kv_multiply(slot)
+        kv_multiply(slot, 0, rows)
         kv_ship(s - 1)
+        return 0
+
+    lax.fori_loop(1, 4, kv_step, 0)
 
     q_weight(0).wait()
     q_weight(2).start()
@@ -473,11 +491,16 @@
         pos0 = base(t)
         nfull = pos0 // KB
         off = pos0 - nfull * KB
-        for blocks in range(seq // KB):
-            for half in range(2):
-                @pl.when(jnp.logical_and(nfull == blocks, off // 256 == half))
-                def _():
-                    run(g, t, slot, off, blocks, (half + 1) * 256)
+        for upper in range(2):
+            @pl.when(nfull // 2 == upper)
+            def _():
+                for low in range(2):
+                    @pl.when(nfull % 2 == low)
+                    def _():
+                        for half in range(2):
+                            @pl.when(off // 256 == half)
+                            def _():
+                                run(g, t, slot, off, 2 * upper + low, (half + 1) * 256)
 
         send_out(slot, t, g)
         return 0

time: 203 us -> 200 us (0.985)
  Pallas kernels: 198 us -> 195 us
    pallas_call x1, Pallas kernels: 72.2 us -> 69.3 us  [front(): pl.pallas_call(front_kernel, in_specs=[ANY, vmem, ANY, ANY, ANY, vmem, vm...]
where the time goes in v2:
time: 200 us
  Pallas kernels  195 us (98%)
  local copies, waits for them, and re-layouts  5.18 us (3%)
    pallas_call x1, Pallas kernels, attention(): pl.pallas_call(attn_kernel, in_specs=[ANY, ANY, ANY], out_specs=[ANY, ANY...  74.7 us
    pallas_call x1, Pallas kernels, front(): pl.pallas_call(front_kernel, in_specs=[ANY, vmem, ANY, ANY, ANY, vmem, vm...  69.3 us
    pallas_call x1, Pallas kernels, out_project(): pl.pallas_call(out_kernel, in_specs=[ANY, ANY, ANY, ANY], out_specs=ANY,...  50.5 us
    unnamed x1, local copies, waits for them, and re-layouts  5.18 us

profile of v2, /device:TPU:3, one launch (start us, length us, event | category | flops | bytes accessed | tf_op | source)
XLA Modules:
  0.0 199.7 jit_solution(7483072796543620070)
XLA Ops:
  0.0 69.3 %front.1 = (bf16[32,1024,256]{2,1,0:T(8,128)(2,1)}, bf16[4,2048,128]{2,1,0:T(8,128)(2,1)}, bf16[4,2048,128]{2,1,0:T(8,128)(2,1)}) custom-call(bf16[512,5120]{1,0:T(8,128)(2,1)} %x_hbm.3, bf16[5120]{0:T(1024)(128)(2,1)} %gain_ref.1, bf16[5120,8192]{1,0:T(8,128)(2,1)} %wq_hbm.1, bf16[5120,1024]{1,0:T(8,128)(2,1)} %wk_hbm.1, bf16[5120,1024]{1,0:T(8,128)(2,1)} %wv_hbm.1, ...), custom_call_target="tpu_custom_call" | custom-call | flops 53687091200 | bytes 41943040 | tf_op jit(solution)/shard_map/front/pallas_call | solution.py:296
  69.3 74.7 %attn.1 = (bf16[512,4096]{1,0:T(8,128)(2,1)}, bf16[512,4096]{1,0:T(8,128)(2,1)}) custom-call(bf16[32,1024,256]{2,1,0:T(8,128)(2,1)} %get-tuple-element.10.q_hbm, bf16[4,2048,128]{2,1,0:T(8,128)(2,1)} %get-tuple-element.11.k_hbm, bf16[4,2048,128]{2,1,0:T(8,128)(2,1)} %get-tuple-element.12.v_hbm), custom_call_target="tpu_custom_call" | custom-call | flops 34359738368 | bytes 25165824 | tf_op jit(solution)/shard_map/attn/pallas_call | solution.py:527
  144.0 50.5 %out_proj.1 = bf16[512,5120]{1,0:T(8,128)(2,1)} custom-call(bf16[512,4096]{1,0:T(8,128)(2,1)} %get-tuple-element.13.keep_hbm, bf16[512,4096]{1,0:T(8,128)(2,1)} %get-tuple-element.14.send_hbm, bf16[8192,5120]{1,0:T(8,128)(2,1)} %wo_hbm.1, bf16[512,5120]{1,0:T(8,128)(2,1)} %x_hbm.3), custom_call_target="tpu_custom_call" | custom-call | flops 42949672960 | bytes 83886080 | tf_op jit(solution)/shard_map/out_proj/pallas_call | solution.py:652
  194.5 5.2 %copy.11 = bf16[512,5120]{1,0:T(8,128)(2,1)} copy(bf16[512,5120]{1,0:T(8,128)(2,1)} %out_proj.1) | data formatting | bytes 10485760

commit v3 on v2

--- a/solution.py
+++ b/solution.py
@@ -58,7 +58,7 @@
         return weight(wq_hbm, core * q_tiles * bn + n * bn, n % 4)
 
     def x_load(i):
-        r = pl.ds(i * part_rows, part_rows)
+        r = pl.ds(pl.multiple_of(i * part_rows, part_rows), part_rows)
         return pltpu.make_async_copy(x_hbm.at[r], own_scr.at[r], x_sems.at[i])
 
     def x_send(i):
@@ -185,14 +185,14 @@
         cos_ref[r, :] = cos_a * cos_b - sin_a * sin_b
         sin_ref[r, :] = sin_a * cos_b + cos_a * sin_b
 
-    for i in range(4):
+    def norm_own(i, _):
         x_load(i).wait()
-
-    def norm_own(i, _):
         norm(own_scr, i)
         return 0
 
     lax.fori_loop(0, 2, norm_own, 0)
+    x_load(2).wait()
+    x_load(3).wait()
     k_weight(0, 0).wait()
     v_weight(0, 1).wait()
     norm(own_scr, 2)

time: 200 us -> 199 us (level)
  no operation moved by 1% of the time
where the time goes in v3:
time: 199 us
  Pallas kernels  194 us (97%)
  local copies, waits for them, and re-layouts  5.18 us (3%)
    pallas_call x1, Pallas kernels, attention(): pl.pallas_call(attn_kernel, in_specs=[ANY, ANY, ANY], out_specs=[ANY, ANY...  74.7 us
    pallas_call x1, Pallas kernels, front(): pl.pallas_call(front_kernel, in_specs=[ANY, vmem, ANY, ANY, ANY, vmem, vm...  68.4 us
    pallas_call x1, Pallas kernels, out_project(): pl.pallas_call(out_kernel, in_specs=[ANY, ANY, ANY, ANY], out_specs=ANY,...  50.5 us
    unnamed x1, local copies, waits for them, and re-layouts  5.18 us

profile of v3, /device:TPU:3, one launch (start us, length us, event | category | flops | bytes accessed | tf_op | source)
XLA Modules:
  0.0 198.8 jit_solution(2880598444812556829)
XLA Ops:
  0.0 68.4 %front.1 = (bf16[32,1024,256]{2,1,0:T(8,128)(2,1)}, bf16[4,2048,128]{2,1,0:T(8,128)(2,1)}, bf16[4,2048,128]{2,1,0:T(8,128)(2,1)}) custom-call(bf16[512,5120]{1,0:T(8,128)(2,1)} %x_hbm.3, bf16[5120]{0:T(1024)(128)(2,1)} %gain_ref.1, bf16[5120,8192]{1,0:T(8,128)(2,1)} %wq_hbm.1, bf16[5120,1024]{1,0:T(8,128)(2,1)} %wk_hbm.1, bf16[5120,1024]{1,0:T(8,128)(2,1)} %wv_hbm.1, ...), custom_call_target="tpu_custom_call" | custom-call | flops 53687091200 | bytes 41943040 | tf_op jit(solution)/shard_map/front/pallas_call | solution.py:296
  68.4 74.7 %attn.1 = (bf16[512,4096]{1,0:T(8,128)(2,1)}, bf16[512,4096]{1,0:T(8,128)(2,1)}) custom-call(bf16[32,1024,256]{2,1,0:T(8,128)(2,1)} %get-tuple-element.10.q_hbm, bf16[4,2048,128]{2,1,0:T(8,128)(2,1)} %get-tuple-element.11.k_hbm, bf16[4,2048,128]{2,1,0:T(8,128)(2,1)} %get-tuple-element.12.v_hbm), custom_call_target="tpu_custom_call" | custom-call | flops 34359738368 | bytes 25165824 | tf_op jit(solution)/shard_map/attn/pallas_call | solution.py:527
  143.1 50.5 %out_proj.1 = bf16[512,5120]{1,0:T(8,128)(2,1)} custom-call(bf16[512,4096]{1,0:T(8,128)(2,1)} %get-tuple-element.13.keep_hbm, bf16[512,4096]{1,0:T(8,128)(2,1)} %get-tuple-element.14.send_hbm, bf16[8192,5120]{1,0:T(8,128)(2,1)} %wo_hbm.1, bf16[512,5120]{1,0:T(8,128)(2,1)} %x_hbm.3), custom_call_target="tpu_custom_call" | custom-call | flops 42949672960 | bytes 83886080 | tf_op jit(solution)/shard_map/out_proj/pallas_call | solution.py:652
  193.6 5.2 %copy.11 = bf16[512,5120]{1,0:T(8,128)(2,1)} copy(bf16[512,5120]{1,0:T(8,128)(2,1)} %out_proj.1) | data formatting | bytes 10485760
